TPU v7x, 32 devices: a whole 2x2x4 slice. The times are simulated.
32 devices in a mesh: seq: 16 (over z, y, x), blk: 2 (over core).
Axes of the slice: x: 2, y: 2, z: 4, core: 2. Of those that a mesh axis runs over, the one named last changes fastest.
Arguments:
- query: bfloat16 [2048, 5120], P(('blk', 'seq')), may hold values from -139 to 139
- keys: bfloat16 [2048, 5120], P(('blk', 'seq')), may hold values from -4.5 to 4.5
- values: bfloat16 [2048, 5120], P(('blk', 'seq')), may hold values from -6 to 6
Outputs:
- attended: bfloat16 [2048, 5120], P(('blk', 'seq'))
All inputs are finite; a program needn't handle non-finite values.
Results may differ from a plain program's by a relative error of at most 0.008.
Values may be sent and summed in bfloat16 or wider, within the bound.
No kernel may reach another device: no remote copies, remote signals or barrier semaphores. Data moves between devices by JAX's collectives and lax.ppermute only.
A program may use at most 64 MiB of HBM per device.

v0:
```python
import jax
import jax.numpy as jnp
from jax import lax
from jax.sharding import PartitionSpec as P

HEADS = 40


def partner(value, axis, bit):
    mask = 2**bit
    pairs = [(source, source ^ mask) for source in range(lax.axis_size(axis))]
    return lax.ppermute(value, axis, pairs)


def partial_block(q_rows, k_tile, v_tile):
    scores = lax.dot_general(
        q_rows, k_tile, (((1,), (1,)), ((), ())), preferred_element_type=jnp.float32
    ) * q_rows.shape[1] ** (-0.5)
    peak = jnp.max(scores, axis=1)
    expo = jnp.exp(scores - peak[:, None])
    totals = jnp.sum(expo, axis=1)
    summed = jnp.dot(expo.astype(jnp.bfloat16), v_tile, preferred_element_type=jnp.float32)
    return (peak, totals, summed)


def combine_parts(left, right):
    peak = jnp.maximum(left[0], right[0])
    scale_left = jnp.exp(left[0] - peak)
    scale_right = jnp.exp(right[0] - peak)
    totals = scale_left * left[1] + scale_right * right[1]
    summed = scale_left[:, None] * left[2] + scale_right[:, None] * right[2]
    return (peak, totals, summed)


def attend_rows(q_rows, first_k, first_v, second_k, second_v):
    state = partial_block(q_rows, first_k, first_v)
    state = combine_parts(state, partial_block(q_rows, second_k, second_v))
    return (state[2] / state[1][:, None]).astype(jnp.bfloat16)


def attend_item(args):
    q_head, first_k, first_v, second_k, second_v = args
    length, width = q_head.shape
    rows = min(512, length)

    def block(q_rows):
        return attend_rows(q_rows, first_k, first_v, second_k, second_v)

    return lax.map(block, q_head.reshape(length // rows, rows, width)).reshape(length, width)


def items_first(array):
    return jnp.transpose(array.reshape(array.shape[0], array.shape[2], array.shape[3]), (1, 0, 2))


def attend_items(pieces):
    q_group, k_group, v_group = pieces
    q_heads = items_first(q_group)
    k_heads = items_first(k_group)
    v_heads = items_first(v_group)
    stacked = jnp.stack([k_heads, v_heads])
    other = partner(stacked, "blk", 0)
    tiles = (q_heads, k_heads, v_heads, other[0], other[1])
    outcome = lax.map(attend_item, tiles)
    count, length, width = outcome.shape
    outcome = jnp.transpose(outcome, (1, 0, 2)).reshape(length, 1, count, width)
    return lax.all_to_all(outcome, "seq", split_axis=0, concat_axis=1, tiled=True)


def on_device(query, keys, values):
    groups = lax.axis_size("seq")
    width = query.shape[1] // HEADS
    tok_rows = query.shape[0]
    key_source, value_source = (keys, values)
    per_dev = (HEADS + groups - 1) // groups
    slots_all = per_dev * groups

    def split_heads(array):
        count_rows = array.shape[0]
        shaped = array.reshape(count_rows, HEADS, width)
        shaped = jnp.pad(shaped, ((0, 0), (0, slots_all - HEADS), (0, 0)))
        return shaped.reshape(count_rows, groups, per_dev, width)

    result = attend_items(
        (
            lax.all_to_all(split_heads(query), "seq", split_axis=1, concat_axis=0, tiled=True),
            lax.all_to_all(split_heads(key_source), "seq", split_axis=1, concat_axis=0, tiled=True),
            lax.all_to_all(
                split_heads(value_source), "seq", split_axis=1, concat_axis=0, tiled=True
            ),
        )
    )
    result = result.reshape(tok_rows, slots_all, width)[:, :HEADS]
    return result.reshape(tok_rows, HEADS * width)


def solution(mesh):
    placed = (P(("blk", "seq"), None), P(("blk", "seq"), None), P(("blk", "seq"), None))
    return jax.shard_map(
        on_device, mesh=mesh, in_specs=placed, out_specs=P(("blk", "seq"), None), check_vma=False
    )
```

profile of v0, /device:TPU:0, one launch (start us, length us, event | category | flops | bytes accessed | tf_op | source)
XLA Modules:
  0.0 155.3 jit_solution(6471587082868300585)
XLA Ops:
  0.0 1.1 copy-done
  1.3 1.0 pad.11.clone
  2.2 8.3 %all-to-all-start.1 = ((bf16[64,16,3,128]{3,0,2,1:T(8,128)(2,1)}), bf16[64,16,3,128]{3,0,2,1:T(8,128)(2,1)S(1)}, u32[]{:S(2)}, u32[]{:S(2)}) async-start(bf16[64,16,3,128]{3,0,2,1:T(8,128)(2,1)} %bitcast.13), calls=%async_computation.1 | async-start | bytes 1572864 | tf_op jit(solution)/shard_map/all_to_all | solution.py:87
  10.8 1.0 pad.12.clone
  11.8 18.5 %all-to-all-done.1 = bf16[64,16,3,128]{3,0,2,1:T(8,128)(2,1)S(1)} async-done(((bf16[64,16,3,128]{3,0,2,1:T(8,128)(2,1)}), bf16[64,16,3,128]{3,0,2,1:T(8,128)(2,1)S(1)}, u32[]{:S(2)}, u32[]{:S(2)}) %all-to-all-start.1) | async-done | bytes 786464 | tf_op jit(solution)/shard_map/all_to_all | solution.py:87
  30.3 5.0 %all-to-all-start.2 = ((bf16[64,16,3,128]{3,0,2,1:T(8,128)(2,1)}), bf16[64,16,3,128]{3,0,2,1:T(8,128)(2,1)S(1)}, u32[]{:S(2)}, u32[]{:S(2)}) async-start(bf16[64,16,3,128]{3,0,2,1:T(8,128)(2,1)} %bitcast.18), calls=%async_computation.2 | async-start | bytes 1572864 | tf_op jit(solution)/shard_map/all_to_all | solution.py:88
  35.3 18.6 %all-to-all-done.2 = bf16[64,16,3,128]{3,0,2,1:T(8,128)(2,1)S(1)} async-done(((bf16[64,16,3,128]{3,0,2,1:T(8,128)(2,1)}), bf16[64,16,3,128]{3,0,2,1:T(8,128)(2,1)S(1)}, u32[]{:S(2)}, u32[]{:S(2)}) %all-to-all-start.2) | async-done | bytes 786464 | tf_op jit(solution)/shard_map/all_to_all | solution.py:88
  53.9 0.9 copy-done.2
  54.8 1.3 copy.18
  56.0 1.3 pad_maximum_fusion
  57.5 1.0 pad.10.clone
  58.5 5.0 %all-to-all-start = ((bf16[64,16,3,128]{3,0,2,1:T(8,128)(2,1)}), bf16[64,16,3,128]{3,0,2,1:T(8,128)(2,1)S(1)}, u32[]{:S(2)}, u32[]{:S(2)}) async-start(bf16[64,16,3,128]{3,0,2,1:T(8,128)(2,1)} %bitcast.121), calls=%async_computation | async-start | bytes 1572864 | tf_op jit(solution)/shard_map/all_to_all | solution.py:86
  63.4 20.1 %all-to-all-done = bf16[64,16,3,128]{3,0,2,1:T(8,128)(2,1)S(1)} async-done(((bf16[64,16,3,128]{3,0,2,1:T(8,128)(2,1)}), bf16[64,16,3,128]{3,0,2,1:T(8,128)(2,1)S(1)}, u32[]{:S(2)}, u32[]{:S(2)}) %all-to-all-start) | async-done | bytes 786464 | tf_op jit(solution)/shard_map/all_to_all | solution.py:86
  83.5 0.9 copy.14
  84.5 2.6 %slice_bitcast_fusion = (bf16[3,1024,128]{2,1,0:T(8,128)(2,1)}, bf16[3,1024,128]{2,1,0:T(8,128)(2,1)}) fusion(bf16[2,3,1024,128]{3,2,1,0:T(8,128)(2,1)} %collective-permute-done), kind=kLoop, calls=%fused_computation.42 | loop fusion | bytes 3145728 | tf_op jit(solution)/shard_map/squeeze | solution.py:63
  87.1 34.5 %while.21 = (s32[]{:T(128)}, bf16[3,1024,128]{2,1,0:T(8,128)(2,1)}, bf16[3,1024,128]{2,1,0:T(8,128)(2,1)}, bf16[3,1024,128]{2,1,0:T(8,128)(2,1)S(1)}, bf16[3,102...) while((s32[]{:T(128)}, bf16[3,1024,128]{2,1,0:T(8,128)(2,1)}, ...), condition=%wide.region_7.8_spmd, body=%wide.region_0.7_spmd.sunk | while | flops 545588224 | bytes 18780980 | solution.py:64
  87.1 1.0 dynamic-slice_bitcast_fusion.6
  88.1 1.7 %dynamic-slice_bitcast_fusion.7 = (bf16[1024,128]{1,0:T(8,128)(2,1)}, bf16[1024,128]{1,0:T(8,128)(2,1)S(1)}) fusion(bf16[3,1024,128]{2,1,0:T(8,128)(2,1)} %get-tuple-element.302, s32[]{:T(128)} %get-tuple-element.286, bf16[3,1024,128]{2,1,0:T(8,128)(2,1)S(1)} %get-tuple-element.300), kind=kLoop, calls=%fused_computation.35.clone.1 | loop fusion | bytes 1048580 | tf_op jit(solution)/shard_map/while/body/jit(dynamic_index_in_dim)/squeeze | solution.py:64
  89.8 1.0 constant_dynamic-slice_fusion.2
  90.8 7.1 %while.22 = (s32[]{:T(128)}, bf16[2,512,128]{2,1,0:T(8,128)(2,1)S(1)}, bf16[2,512,128]{2,1,0:T(8,128)(2,1)S(1)}, bf16[1024,128]{1,0:T(8,128)(2,1)S(1)}, bf16[102...) while((s32[]{:T(128)}, ...), condition=%wide.region_6.6_spmd, body=%wide.region_1.5_spmd.sunk | while | flops 545588224 | bytes 15634557 | solution.py:49
  90.8 0.5 multiply_reduce_fusion.4
  91.3 0.5 multiply_reduce_fusion.5
  91.8 1.0 fusion.50
  92.8 0.5 convolution_multiply_fusion.3
  93.7 0.6 fusion.51
  94.3 0.5 multiply_reduce_fusion.4
  94.9 0.5 multiply_reduce_fusion.5
  95.4 1.0 fusion.50
  96.4 0.5 convolution_multiply_fusion.3
  97.3 0.6 fusion.51
  97.9 0.7 bitcast_dynamic-update-slice_fusion.2
  98.6 1.0 dynamic-slice_bitcast_fusion.6
  99.6 1.7 %dynamic-slice_bitcast_fusion.7 = (bf16[1024,128]{1,0:T(8,128)(2,1)}, bf16[1024,128]{1,0:T(8,128)(2,1)S(1)}) fusion(bf16[3,1024,128]{2,1,0:T(8,128)(2,1)} %get-tuple-element.302, s32[]{:T(128)} %get-tuple-element.286, bf16[3,1024,128]{2,1,0:T(8,128)(2,1)S(1)} %get-tuple-element.300), kind=kLoop, calls=%fused_computation.35.clone.1 | loop fusion | bytes 1048580 | tf_op jit(solution)/shard_map/while/body/jit(dynamic_index_in_dim)/squeeze | solution.py:64
  101.3 1.0 constant_dynamic-slice_fusion.2
  102.3 7.1 %while.22 = (s32[]{:T(128)}, bf16[2,512,128]{2,1,0:T(8,128)(2,1)S(1)}, bf16[2,512,128]{2,1,0:T(8,128)(2,1)S(1)}, bf16[1024,128]{1,0:T(8,128)(2,1)S(1)}, bf16[102...) while((s32[]{:T(128)}, ...), condition=%wide.region_6.6_spmd, body=%wide.region_1.5_spmd.sunk | while | flops 545588224 | bytes 15634557 | solution.py:49
  102.3 0.5 multiply_reduce_fusion.4
  102.8 0.5 multiply_reduce_fusion.5
  103.3 1.0 fusion.50
  104.3 0.5 convolution_multiply_fusion.3
  105.2 0.6 fusion.51
  105.8 0.5 multiply_reduce_fusion.4
  106.3 0.5 multiply_reduce_fusion.5
  106.9 1.0 fusion.50
  107.8 0.5 convolution_multiply_fusion.3
  108.8 0.6 fusion.51
  109.4 0.7 bitcast_dynamic-update-slice_fusion.2
  110.1 1.0 dynamic-slice_bitcast_fusion.6
  111.1 1.7 %dynamic-slice_bitcast_fusion.7 = (bf16[1024,128]{1,0:T(8,128)(2,1)}, bf16[1024,128]{1,0:T(8,128)(2,1)S(1)}) fusion(bf16[3,1024,128]{2,1,0:T(8,128)(2,1)} %get-tuple-element.302, s32[]{:T(128)} %get-tuple-element.286, bf16[3,1024,128]{2,1,0:T(8,128)(2,1)S(1)} %get-tuple-element.300), kind=kLoop, calls=%fused_computation.35.clone.1 | loop fusion | bytes 1048580 | tf_op jit(solution)/shard_map/while/body/jit(dynamic_index_in_dim)/squeeze | solution.py:64
  112.8 1.0 constant_dynamic-slice_fusion.2
  113.8 7.1 %while.22 = (s32[]{:T(128)}, bf16[2,512,128]{2,1,0:T(8,128)(2,1)S(1)}, bf16[2,512,128]{2,1,0:T(8,128)(2,1)S(1)}, bf16[1024,128]{1,0:T(8,128)(2,1)S(1)}, bf16[102...) while((s32[]{:T(128)}, ...), condition=%wide.region_6.6_spmd, body=%wide.region_1.5_spmd.sunk | while | flops 545588224 | bytes 15634557 | solution.py:49
  113.8 0.5 multiply_reduce_fusion.4
  114.3 0.5 multiply_reduce_fusion.5
  114.8 1.0 fusion.50
  115.8 0.5 convolution_multiply_fusion.3
  116.7 0.6 fusion.51
  117.3 0.5 multiply_reduce_fusion.4
  117.8 0.5 multiply_reduce_fusion.5
  118.4 1.0 fusion.50
  119.3 0.5 convolution_multiply_fusion.3
  120.3 0.6 fusion.51
  120.9 0.7 bitcast_dynamic-update-slice_fusion.2
  121.6 1.8 %copy.35 = bf16[3,1024,128]{2,0,1:T(4,128)(2,1)S(1)} copy(bf16[3,1024,128]{2,1,0:T(8,128)(2,1)} %get-tuple-element.79) | data formatting | bytes 1572864 | tf_op jit(solution)/shard_map/while | solution.py:64
  123.4 30.8 %all_to_all.60 = bf16[1024,1,3,128]{3,2,1,0:T(4,128)(2,1)S(1)} all-to-all(bf16[1024,1,3,128]{3,2,1,0:T(4,128)(2,1)S(1)} %bitcast.116), channel_id=1, replica_groups=mesh['seq'=16,'blk'=2] {'seq'}, dimensions={0} | all-to-all | bytes 1572864 | tf_op jit(solution)/shard_map/all_to_all | solution.py:67
  154.4 0.9 copy_bitcast_fusion.1
  (36 shorter events, 3.2 us)
Async XLA Ops:
  0.0 1.1 copy-start
  0.0 10.6 %copy-start.3 = (bf16[64,5120]{1,0:T(8,128)(2,1)S(1)}, bf16[64,5120]{1,0:T(8,128)(2,1)}, u32[]{:S(2)}) copy-start(bf16[64,5120]{1,0:T(8,128)(2,1)} %param.9) | copy-start | bytes 1966084
  2.2 28.0 %all-to-all-start.1 = ((bf16[64,16,3,128]{3,0,2,1:T(8,128)(2,1)}), bf16[64,16,3,128]{3,0,2,1:T(8,128)(2,1)S(1)}, u32[]{:S(2)}, u32[]{:S(2)}) async-start(bf16[64,16,3,128]{3,0,2,1:T(8,128)(2,1)} %bitcast.13), calls=%async_computation.1 | async-start | bytes 1572864 | tf_op jit(solution)/shard_map/all_to_all | solution.py:87
  30.3 23.6 %all-to-all-start.2 = ((bf16[64,16,3,128]{3,0,2,1:T(8,128)(2,1)}), bf16[64,16,3,128]{3,0,2,1:T(8,128)(2,1)S(1)}, u32[]{:S(2)}, u32[]{:S(2)}) async-start(bf16[64,16,3,128]{3,0,2,1:T(8,128)(2,1)} %bitcast.18), calls=%async_computation.2 | async-start | bytes 1572864 | tf_op jit(solution)/shard_map/all_to_all | solution.py:88
  53.9 0.9 copy-start.2
  54.8 2.6 %copy-start.4 = (bf16[64,5120]{1,0:T(8,128)(2,1)S(1)}, bf16[64,5120]{1,0:T(8,128)(2,1)}, u32[]{:S(2)}) copy-start(bf16[64,5120]{1,0:T(8,128)(2,1)} %param.7) | copy-start | bytes 1966084
  57.3 27.2 %collective-permute-start = (bf16[2,3,1024,128]{3,2,1,0:T(8,128)(2,1)}, bf16[2,3,1024,128]{3,2,1,0:T(8,128)(2,1)}, u32[]{:S(2)}, u32[]{:S(2)}) collective-permute-start(bf16[2,3,1024,128]{3,2,1,0:T(8,128)(2,1)} %pad_maximum_fusion), channel_id=1, source_target_pairs={{0,1},{1,0},{2,3},{3,2},{4,5},{5,4},{6,7},{7,6},{8,9},{9,8},{10,11... | collective-permute-start | bytes 4718600 | tf_op jit(solution)/shard_map/ppermute | solution.py:12
  58.5 25.1 %all-to-all-start = ((bf16[64,16,3,128]{3,0,2,1:T(8,128)(2,1)}), bf16[64,16,3,128]{3,0,2,1:T(8,128)(2,1)S(1)}, u32[]{:S(2)}, u32[]{:S(2)}) async-start(bf16[64,16,3,128]{3,0,2,1:T(8,128)(2,1)} %bitcast.121), calls=%async_computation | async-start | bytes 1572864 | tf_op jit(solution)/shard_map/all_to_all | solution.py:86
  92.8 1.0 copy-start.1
  96.3 1.0 copy-start.1
  104.3 1.0 copy-start.1
  107.8 1.0 copy-start.1
  115.8 1.0 copy-start.1
  119.3 1.0 copy-start.1
where the time goes:
time: 156 us; the launch traced here: 155 us
  waiting for transfers between devices  57.1 us (37%)
  blocking collectives  30.8 us (20%)
  local copies, waits for them, and re-layouts  28.7 us (18%)
  starting transfers between devices  18.2 us (12%)
  matrix products  12.9 us (8%)
  other arithmetic  7.11 us (5%)
    all_to_all x1, blocking collectives, attend_items(): lax.all_to_all(outcome, 'seq', split_axis=0, concat_axis=1, tiled=True)  30.8 us
    all_to_all x1, waiting for transfers between devices, on_device(): lax.all_to_all(split_heads(query), 'seq', split_axis=1, concat_axis=0, ti...  20.1 us
    all_to_all x1, waiting for transfers between devices, on_device(): lax.all_to_all(split_heads(value_source), 'seq', split_axis=1, concat_axi...  18.6 us
    all_to_all x1, waiting for transfers between devices, on_device(): lax.all_to_all(split_heads(key_source), 'seq', split_axis=1, concat_axis=...  18.5 us
    all_to_all x1, starting transfers between devices, on_device(): lax.all_to_all(split_heads(key_source), 'seq', split_axis=1, concat_axis=...  8.34 us
    squeeze x6, local copies, waits for them, and re-layouts, attend_items(): outcome = lax.map(attend_item, tiles)  8.03 us
    dot_general x12, matrix products, partial_block(): jnp.dot(expo.astype(jnp.bfloat16), v_tile, preferred_element_type=jnp.flo...  6.67 us
    dot_general x12, matrix products, partial_block(): lax.dot_general(q_rows, k_tile, (((1,), (1,)), ((), ())), preferred_eleme...  6.23 us
  transfers between devices with their start and end apart: 4, of which 3 were waited for; matrix products, arithmetic and copies ran while one was open for 2% of the time, Pallas kernels for 0%

commit v1 on v0

--- a/solution.py
+++ b/solution.py
@@ -4,6 +4,22 @@
 from jax.sharding import PartitionSpec as P
 
 HEADS = 40
+
+
+def swapped_with_each(array, axis, split, join):
+    ways, here = (lax.axis_size(axis), lax.axis_index(axis))
+    width = array.shape[split] // ways
+    shape = list(array.shape)
+    shape[split] = width
+    height = shape[join]
+    shape[join] = height * ways
+    full = jnp.zeros(shape, array.dtype)
+    for mask in range(ways):
+        part = lax.dynamic_slice_in_dim(array, (here ^ mask) * width, width, axis=split)
+        if mask:
+            part = lax.ppermute(part, axis, [(d, d ^ mask) for d in range(ways)])
+        full = lax.dynamic_update_slice_in_dim(full, part, (here ^ mask) * height, axis=join)
+    return full
 
 
 def partner(value, axis, bit):
@@ -83,7 +99,7 @@
 
     result = attend_items(
         (
-            lax.all_to_all(split_heads(query), "seq", split_axis=1, concat_axis=0, tiled=True),
+            swapped_with_each(split_heads(query), "seq", 1, 0),
             lax.all_to_all(split_heads(key_source), "seq", split_axis=1, concat_axis=0, tiled=True),
             lax.all_to_all(
                 split_heads(value_source), "seq", split_axis=1, concat_axis=0, tiled=True

time: 156 us -> 146 us (0.936)
  waiting for transfers between devices: 57.1 us -> 16 us
  starting transfers between devices: 18.2 us -> 41.4 us
  local copies, waits for them, and re-layouts: 28.7 us -> 39.6 us
  blocking collectives: 30.8 us -> 28.4 us
    ppermute x0 -> x15, starting transfers between devices: none -> 27.9 us  [swapped_with_each(): part = lax.ppermute(part, axis, [(d, d ^ mask) for d in range(ways)])]
    all_to_all x1 -> x0, waiting for transfers between devices: 20.1 us -> none  [on_device(): lax.all_to_all(split_heads(query), 'seq', split_axis=1, concat_axis=0, ti...]
    all_to_all x1, waiting for transfers between devices: 18.6 us -> 0.01 us  [on_device(): lax.all_to_all(split_heads(value_source), 'seq', split_axis=1, concat_axi...]
    dynamic_update_slice x0 -> x16, local copies, waits for them, and re-layouts: none -> 14.1 us  [swapped_with_each(): lax.dynamic_update_slice_in_dim(full, part, (here ^ mask) * height, axis=...]
    all_to_all x1, waiting for transfers between devices: 18.5 us -> 4.44 us  [on_device(): lax.all_to_all(split_heads(key_source), 'seq', split_axis=1, concat_axis=...]
    ppermute x0 -> x15, waiting for transfers between devices: none -> 11.6 us  [swapped_with_each(): part = lax.ppermute(part, axis, [(d, d ^ mask) for d in range(ways)])]
    all_to_all x1 -> x0, starting transfers between devices: 4.95 us -> none  [on_device(): lax.all_to_all(split_heads(query), 'seq', split_axis=1, concat_axis=0, ti...]
    all_to_all x1, blocking collectives: 30.8 us -> 28.4 us  [attend_items(): lax.all_to_all(outcome, 'seq', split_axis=0, concat_axis=1, tiled=True)]
  transfers between devices with their start and end apart: 4 -> 18, of which waited for: 3 -> 3; matrix products, arithmetic and copies ran while one was open for 2% -> 12% of each run, Pallas kernels for 0% -> 0%
where the time goes in v1:
time: 146 us; the launch traced here: 145 us
  starting transfers between devices  41.4 us (28%)
  local copies, waits for them, and re-layouts  39.6 us (27%)
  blocking collectives  28.4 us (19%)
  waiting for transfers between devices  16 us (11%)
  matrix products  12.9 us (9%)
  other arithmetic  6.02 us (4%)
    all_to_all x1, blocking collectives, attend_items(): lax.all_to_all(outcome, 'seq', split_axis=0, concat_axis=1, tiled=True)  28.4 us
    ppermute x15, starting transfers between devices, swapped_with_each(): part = lax.ppermute(part, axis, [(d, d ^ mask) for d in range(ways)])  27.9 us
    dynamic_update_slice x16, local copies, waits for them, and re-layouts, swapped_with_each(): lax.dynamic_update_slice_in_dim(full, part, (here ^ mask) * height, axis=...  14.1 us
    ppermute x15, waiting for transfers between devices, swapped_with_each(): part = lax.ppermute(part, axis, [(d, d ^ mask) for d in range(ways)])  11.6 us
    all_to_all x1, starting transfers between devices, on_device(): lax.all_to_all(split_heads(key_source), 'seq', split_axis=1, concat_axis=...  8.34 us
    squeeze x6, local copies, waits for them, and re-layouts, attend_items(): outcome = lax.map(attend_item, tiles)  8.03 us
    dot_general x12, matrix products, partial_block(): jnp.dot(expo.astype(jnp.bfloat16), v_tile, preferred_element_type=jnp.flo...  6.66 us
    dot_general x12, matrix products, partial_block(): lax.dot_general(q_rows, k_tile, (((1,), (1,)), ((), ())), preferred_eleme...  6.23 us
  transfers between devices with their start and end apart: 18, of which 3 were waited for; matrix products, arithmetic and copies ran while one was open for 12% of the time, Pallas kernels for 0%

profile of v1, /device:TPU:0, one launch (start us, length us, event | category | flops | bytes accessed | tf_op | source)
XLA Modules:
  0.0 145.0 jit_solution(9687961356207367418)
XLA Ops:
  0.0 1.1 copy-done
  1.3 1.0 pad.11.clone
  2.3 8.3 %all-to-all-start = ((bf16[64,16,3,128]{3,0,2,1:T(8,128)(2,1)}), bf16[64,16,3,128]{3,0,2,1:T(8,128)(2,1)S(1)}, u32[]{:S(2)}, u32[]{:S(2)}) async-start(bf16[64,16,3,128]{3,0,2,1:T(8,128)(2,1)} %bitcast.26), calls=%async_computation | async-start | bytes 1572864 | tf_op jit(solution)/shard_map/all_to_all | solution.py:103
  11.1 0.9 constant_dynamic-slice_fusion.1
  12.0 1.9 %collective-permute-start = (bf16[64,1,3,128]{3,0,2,1:T(8,128)(2,1)}, bf16[64,1,3,128]{3,0,2,1:T(8,128)(2,1)}, u32[]{:S(2)}, u32[]{:S(2)}) collective-permute-start(bf16[64,1,3,128]{3,0,2,1:T(8,128)(2,1)} %get-tuple-element.137), channel_id=1, source_target_pairs={{0,2},{2,0},{4,6},{6,4},{8,10},{10,8},{12,14},{14,12},{16,18},{18,... | collective-permute-start | bytes 147464 | tf_op jit(solution)/shard_map/ppermute | solution.py:20
  13.9 1.5 %collective-permute-start.1 = (bf16[64,1,3,128]{3,0,2,1:T(8,128)(2,1)}, bf16[64,1,3,128]{3,0,2,1:T(8,128)(2,1)}, u32[]{:S(2)}, u32[]{:S(2)}) collective-permute-start(bf16[64,1,3,128]{3,0,2,1:T(8,128)(2,1)} %get-tuple-element.136), channel_id=1, source_target_pairs={{0,4},{2,6},{4,0},{6,2},{8,12},{10,14},{12,8},{14,10},{16,20},{18,... | collective-permute-start | bytes 147464 | tf_op jit(solution)/shard_map/ppermute | solution.py:20
  15.5 1.9 %collective-permute-start.3 = (bf16[64,1,3,128]{3,0,2,1:T(8,128)(2,1)}, bf16[64,1,3,128]{3,0,2,1:T(8,128)(2,1)}, u32[]{:S(2)}, u32[]{:S(2)}) collective-permute-start(bf16[64,1,3,128]{3,0,2,1:T(8,128)(2,1)} %get-tuple-element.134), channel_id=1, source_target_pairs={{0,8},{2,10},{4,12},{6,14},{8,0},{10,2},{12,4},{14,6},{16,24},{18,... | collective-permute-start | bytes 147464 | tf_op jit(solution)/shard_map/ppermute | solution.py:20
  17.4 1.5 %collective-permute-start.4 = (bf16[64,1,3,128]{3,0,2,1:T(8,128)(2,1)}, bf16[64,1,3,128]{3,0,2,1:T(8,128)(2,1)}, u32[]{:S(2)}, u32[]{:S(2)}) collective-permute-start(bf16[64,1,3,128]{3,0,2,1:T(8,128)(2,1)} %get-tuple-element.133), channel_id=1, source_target_pairs={{0,10},{2,8},{4,14},{6,12},{8,2},{10,0},{12,6},{14,4},{16,26},{18,... | collective-permute-start | bytes 147464 | tf_op jit(solution)/shard_map/ppermute | solution.py:20
  19.1 1.0 reshape.135
  20.1 0.6 bitcast_dynamic-update-slice_fusion.16
  20.7 1.0 pad.12.clone
  21.8 2.4 %collective-permute-start.5 = (bf16[64,1,3,128]{3,0,2,1:T(8,128)(2,1)S(1)}, bf16[64,1,3,128]{3,0,2,1:T(8,128)(2,1)S(1)}, u32[]{:S(2)}, u32[]{:S(2)}) collective-permute-start(bf16[64,1,3,128]{3,0,2,1:T(8,128)(2,1)S(1)} %copy-done.13), channel_id=1, source_target_pairs={{0,12},{2,14},{4,8},{6,10},{8,4},{10,6},{12,0},{14,2},{16,28},{18,... | collective-permute-start | bytes 147464 | tf_op jit(solution)/shard_map/ppermute | solution.py:20
  24.1 1.4 bitcast_dynamic-update-slice_fusion.15
  25.7 4.4 %all-to-all-done = bf16[64,16,3,128]{3,0,2,1:T(8,128)(2,1)S(1)} async-done(((bf16[64,16,3,128]{3,0,2,1:T(8,128)(2,1)}), bf16[64,16,3,128]{3,0,2,1:T(8,128)(2,1)S(1)}, u32[]{:S(2)}, u32[]{:S(2)}) %all-to-all-start) | async-done | bytes 786464 | tf_op jit(solution)/shard_map/all_to_all | solution.py:103
  30.2 5.1 %all-to-all-start.1 = ((bf16[64,16,3,128]{3,0,2,1:T(8,128)(2,1)}), bf16[64,16,3,128]{3,0,2,1:T(8,128)(2,1)S(1)}, u32[]{:S(2)}, u32[]{:S(2)}) async-start(bf16[64,16,3,128]{3,0,2,1:T(8,128)(2,1)} %bitcast.31), calls=%async_computation.1 | async-start | bytes 1572864 | tf_op jit(solution)/shard_map/all_to_all | solution.py:104
  35.3 1.4 bitcast_dynamic-update-slice_fusion.14
  36.7 2.8 %collective-permute-start.7 = (bf16[64,1,3,128]{3,0,2,1:T(8,128)(2,1)S(1)}, bf16[64,1,3,128]{3,0,2,1:T(8,128)(2,1)S(1)}, u32[]{:S(2)}, u32[]{:S(2)}) collective-permute-start(bf16[64,1,3,128]{3,0,2,1:T(8,128)(2,1)S(1)} %copy-done.11), channel_id=1, source_target_pairs={{0,16},{2,18},{4,20},{6,22},{8,24},{10,26},{12,28},{14,30},{16,0},... | collective-permute-start | bytes 147464 | tf_op jit(solution)/shard_map/ppermute | solution.py:20
  39.6 1.4 bitcast_dynamic-update-slice_fusion.13
  41.0 1.5 %collective-permute-start.8 = (bf16[64,1,3,128]{3,0,2,1:T(8,128)(2,1)S(1)}, bf16[64,1,3,128]{3,0,2,1:T(8,128)(2,1)S(1)}, u32[]{:S(2)}, u32[]{:S(2)}) collective-permute-start(bf16[64,1,3,128]{3,0,2,1:T(8,128)(2,1)S(1)} %copy-done.10), channel_id=1, source_target_pairs={{0,18},{2,16},{4,22},{6,20},{8,26},{10,24},{12,30},{14,28},{16,2},... | collective-permute-start | bytes 147464 | tf_op jit(solution)/shard_map/ppermute | solution.py:20
  42.5 1.4 bitcast_dynamic-update-slice_fusion.12
  43.9 3.3 %collective-permute-start.9 = (bf16[64,1,3,128]{3,0,2,1:T(8,128)(2,1)S(1)}, bf16[64,1,3,128]{3,0,2,1:T(8,128)(2,1)S(1)}, u32[]{:S(2)}, u32[]{:S(2)}) collective-permute-start(bf16[64,1,3,128]{3,0,2,1:T(8,128)(2,1)S(1)} %copy-done.9), channel_id=1, source_target_pairs={{0,20},{2,22},{4,16},{6,18},{8,28},{10,30},{12,24},{14,26},{16,4},... | collective-permute-start | bytes 147464 | tf_op jit(solution)/shard_map/ppermute | solution.py:20
  47.2 1.4 bitcast_dynamic-update-slice_fusion.11
  48.7 0.6 bitcast_dynamic-update-slice_fusion.10
  49.3 3.7 %collective-permute-start.11 = (bf16[64,1,3,128]{3,0,2,1:T(8,128)(2,1)S(1)}, bf16[64,1,3,128]{3,0,2,1:T(8,128)(2,1)S(1)}, u32[]{:S(2)}, u32[]{:S(2)}) collective-permute-start(bf16[64,1,3,128]{3,0,2,1:T(8,128)(2,1)S(1)} %copy-done.7), channel_id=1, source_target_pairs={{0,24},{2,26},{4,28},{6,30},{8,16},{10,18},{12,20},{14,22},{16,8},... | collective-permute-start | bytes 147464 | tf_op jit(solution)/shard_map/ppermute | solution.py:20
  53.1 0.6 bitcast_dynamic-update-slice_fusion.9
  53.7 7.9 %collective-permute-done.7 = bf16[64,1,3,128]{3,0,2,1:T(8,128)(2,1)S(1)} collective-permute-done((bf16[64,1,3,128]{3,0,2,1:T(8,128)(2,1)S(1)}, bf16[64,1,3,128]{3,0,2,1:T(8,128)(2,1)S(1)}, u32[]{:S(2)}, u32[]{:S(2)}) %collective-permute-start.7) | collective-permute-done | bytes 49184 | tf_op jit(solution)/shard_map/ppermute | solution.py:20
  61.6 2.5 %collective-permute-start.12 = (bf16[64,1,3,128]{3,0,2,1:T(8,128)(2,1)S(1)}, bf16[64,1,3,128]{3,0,2,1:T(8,128)(2,1)S(1)}, u32[]{:S(2)}, u32[]{:S(2)}) collective-permute-start(bf16[64,1,3,128]{3,0,2,1:T(8,128)(2,1)S(1)} %copy-done.6), channel_id=1, source_target_pairs={{0,26},{2,24},{4,30},{6,28},{8,18},{10,16},{12,22},{14,20},{16,10}... | collective-permute-start | bytes 147464 | tf_op jit(solution)/shard_map/ppermute | solution.py:20
  64.1 0.6 bitcast_dynamic-update-slice_fusion.8
  65.1 0.6 bitcast_dynamic-update-slice_fusion.7
  65.8 3.1 %collective-permute-start.13 = (bf16[64,1,3,128]{3,0,2,1:T(8,128)(2,1)S(1)}, bf16[64,1,3,128]{3,0,2,1:T(8,128)(2,1)S(1)}, u32[]{:S(2)}, u32[]{:S(2)}) collective-permute-start(bf16[64,1,3,128]{3,0,2,1:T(8,128)(2,1)S(1)} %copy-done.5), channel_id=1, source_target_pairs={{0,28},{2,30},{4,24},{6,26},{8,20},{10,22},{12,16},{14,18},{16,12}... | collective-permute-start | bytes 147464 | tf_op jit(solution)/shard_map/ppermute | solution.py:20
  68.9 0.6 bitcast_dynamic-update-slice_fusion.6
  69.5 1.5 %collective-permute-start.14 = (bf16[64,1,3,128]{3,0,2,1:T(8,128)(2,1)S(1)}, bf16[64,1,3,128]{3,0,2,1:T(8,128)(2,1)S(1)}, u32[]{:S(2)}, u32[]{:S(2)}) collective-permute-start(bf16[64,1,3,128]{3,0,2,1:T(8,128)(2,1)S(1)} %copy-done.4), channel_id=1, source_target_pairs={{0,30},{2,28},{4,26},{6,24},{8,22},{10,20},{12,18},{14,16},{16,14}... | collective-permute-start | bytes 147464 | tf_op jit(solution)/shard_map/ppermute | solution.py:20
  71.1 0.6 bitcast_dynamic-update-slice_fusion.5
  71.7 0.6 bitcast_dynamic-update-slice_fusion.4
  72.3 0.6 bitcast_dynamic-update-slice_fusion.3
  72.9 0.6 bitcast_dynamic-update-slice_fusion.2
  73.6 3.7 %collective-permute-done.14 = bf16[64,1,3,128]{3,0,2,1:T(8,128)(2,1)S(1)} collective-permute-done((bf16[64,1,3,128]{3,0,2,1:T(8,128)(2,1)S(1)}, bf16[64,1,3,128]{3,0,2,1:T(8,128)(2,1)S(1)}, u32[]{:S(2)}, u32[]{:S(2)}) %collective-permute-start.14) | collective-permute-done | bytes 49184 | tf_op jit(solution)/shard_map/ppermute | solution.py:20
  77.2 0.6 bitcast_dynamic-update-slice_fusion.1
  77.9 1.3 slice_bitcast_fusion
  79.1 34.6 %while.21 = (s32[]{:T(128)}, bf16[3,1024,128]{2,1,0:T(8,128)(2,1)}, bf16[3,1024,128]{2,1,0:T(8,128)(2,1)}, bf16[3,1024,128]{2,1,0:T(8,128)(2,1)S(1)}, bf16[3,102...) while((s32[]{:T(128)}, bf16[3,1024,128]{2,1,0:T(8,128)(2,1)}, ...), condition=%wide.region_7.8_spmd, body=%wide.region_0.7_spmd.sunk | while | flops 545588224 | bytes 18780980 | solution.py:80
  79.1 1.0 dynamic-slice_bitcast_fusion.6
  80.1 1.7 %dynamic-slice_bitcast_fusion.7 = (bf16[1024,128]{1,0:T(8,128)(2,1)}, bf16[1024,128]{1,0:T(8,128)(2,1)S(1)}) fusion(bf16[3,1024,128]{2,1,0:T(8,128)(2,1)} %get-tuple-element.317, s32[]{:T(128)} %get-tuple-element.301, bf16[3,1024,128]{2,1,0:T(8,128)(2,1)S(1)} %get-tuple-element.315), kind=kLoop, calls=%fused_computation.35.clone.1 | loop fusion | bytes 1048580 | tf_op jit(solution)/shard_map/while/body/jit(dynamic_index_in_dim)/squeeze | solution.py:80
  81.8 1.0 constant_dynamic-slice_fusion.17
  82.8 7.1 %while.22 = (s32[]{:T(128)}, bf16[2,512,128]{2,1,0:T(8,128)(2,1)S(1)}, bf16[2,512,128]{2,1,0:T(8,128)(2,1)S(1)}, bf16[1024,128]{1,0:T(8,128)(2,1)S(1)}, bf16[102...) while((s32[]{:T(128)}, ...), condition=%wide.region_6.6_spmd, body=%wide.region_1.5_spmd.sunk | while | flops 545588224 | bytes 15634557 | solution.py:65
  83.8 1.0 fusion.50
  87.4 1.0 fusion.50
  89.9 0.7 bitcast_dynamic-update-slice_fusion.18
  90.6 1.0 dynamic-slice_bitcast_fusion.6
  91.6 1.7 %dynamic-slice_bitcast_fusion.7 = (bf16[1024,128]{1,0:T(8,128)(2,1)}, bf16[1024,128]{1,0:T(8,128)(2,1)S(1)}) fusion(bf16[3,1024,128]{2,1,0:T(8,128)(2,1)} %get-tuple-element.317, s32[]{:T(128)} %get-tuple-element.301, bf16[3,1024,128]{2,1,0:T(8,128)(2,1)S(1)} %get-tuple-element.315), kind=kLoop, calls=%fused_computation.35.clone.1 | loop fusion | bytes 1048580 | tf_op jit(solution)/shard_map/while/body/jit(dynamic_index_in_dim)/squeeze | solution.py:80
  93.3 1.0 constant_dynamic-slice_fusion.17
  94.3 7.1 %while.22 = (s32[]{:T(128)}, bf16[2,512,128]{2,1,0:T(8,128)(2,1)S(1)}, bf16[2,512,128]{2,1,0:T(8,128)(2,1)S(1)}, bf16[1024,128]{1,0:T(8,128)(2,1)S(1)}, bf16[102...) while((s32[]{:T(128)}, ...), condition=%wide.region_6.6_spmd, body=%wide.region_1.5_spmd.sunk | while | flops 545588224 | bytes 15634557 | solution.py:65
  95.3 1.0 fusion.50
  98.9 1.0 fusion.50
  101.4 0.7 bitcast_dynamic-update-slice_fusion.18
  102.2 1.0 dynamic-slice_bitcast_fusion.6
  103.1 1.7 %dynamic-slice_bitcast_fusion.7 = (bf16[1024,128]{1,0:T(8,128)(2,1)}, bf16[1024,128]{1,0:T(8,128)(2,1)S(1)}) fusion(bf16[3,1024,128]{2,1,0:T(8,128)(2,1)} %get-tuple-element.317, s32[]{:T(128)} %get-tuple-element.301, bf16[3,1024,128]{2,1,0:T(8,128)(2,1)S(1)} %get-tuple-element.315), kind=kLoop, calls=%fused_computation.35.clone.1 | loop fusion | bytes 1048580 | tf_op jit(solution)/shard_map/while/body/jit(dynamic_index_in_dim)/squeeze | solution.py:80
  104.8 1.0 constant_dynamic-slice_fusion.17
  105.8 7.1 %while.22 = (s32[]{:T(128)}, bf16[2,512,128]{2,1,0:T(8,128)(2,1)S(1)}, bf16[2,512,128]{2,1,0:T(8,128)(2,1)S(1)}, bf16[1024,128]{1,0:T(8,128)(2,1)S(1)}, bf16[102...) while((s32[]{:T(128)}, ...), condition=%wide.region_6.6_spmd, body=%wide.region_1.5_spmd.sunk | while | flops 545588224 | bytes 15634557 | solution.py:65
  106.9 1.0 fusion.50
  110.4 1.0 fusion.50
  112.9 0.7 bitcast_dynamic-update-slice_fusion.18
  113.7 1.8 %copy.34 = bf16[3,1024,128]{2,0,1:T(4,128)(2,1)S(1)} copy(bf16[3,1024,128]{2,1,0:T(8,128)(2,1)} %get-tuple-element.79) | data formatting | bytes 1572864 | tf_op jit(solution)/shard_map/while | solution.py:80
  115.5 28.4 %all_to_all.45 = bf16[1024,1,3,128]{3,2,1,0:T(4,128)(2,1)S(1)} all-to-all(bf16[1024,1,3,128]{3,2,1,0:T(4,128)(2,1)S(1)} %bitcast.142), channel_id=1, replica_groups=mesh['seq'=16,'blk'=2] {'seq'}, dimensions={0} | all-to-all | bytes 1572864 | tf_op jit(solution)/shard_map/all_to_all | solution.py:83
  144.1 0.9 copy_bitcast_fusion.1
  (99 shorter events, 17.0 us)
Async XLA Ops:
  0.0 1.1 copy-start
  0.0 10.7 %copy-start.2 = (bf16[64,5120]{1,0:T(8,128)(2,1)S(1)}, bf16[64,5120]{1,0:T(8,128)(2,1)}, u32[]{:S(2)}) copy-start(bf16[64,5120]{1,0:T(8,128)(2,1)} %param.7) | copy-start | bytes 1966084
  2.3 27.9 %all-to-all-start = ((bf16[64,16,3,128]{3,0,2,1:T(8,128)(2,1)}), bf16[64,16,3,128]{3,0,2,1:T(8,128)(2,1)S(1)}, u32[]{:S(2)}, u32[]{:S(2)}) async-start(bf16[64,16,3,128]{3,0,2,1:T(8,128)(2,1)} %bitcast.26), calls=%async_computation | async-start | bytes 1572864 | tf_op jit(solution)/shard_map/all_to_all | solution.py:103
  10.7 8.1 %copy-start.3 = (bf16[64,5120]{1,0:T(8,128)(2,1)S(1)}, bf16[64,5120]{1,0:T(8,128)(2,1)}, u32[]{:S(2)}) copy-start(bf16[64,5120]{1,0:T(8,128)(2,1)} %param.9) | copy-start | bytes 1966084
  12.0 9.7 %collective-permute-start = (bf16[64,1,3,128]{3,0,2,1:T(8,128)(2,1)}, bf16[64,1,3,128]{3,0,2,1:T(8,128)(2,1)}, u32[]{:S(2)}, u32[]{:S(2)}) collective-permute-start(bf16[64,1,3,128]{3,0,2,1:T(8,128)(2,1)} %get-tuple-element.137), channel_id=1, source_target_pairs={{0,2},{2,0},{4,6},{6,4},{8,10},{10,8},{12,14},{14,12},{16,18},{18,... | collective-permute-start | bytes 147464 | tf_op jit(solution)/shard_map/ppermute | solution.py:20
  13.9 11.7 %collective-permute-start.1 = (bf16[64,1,3,128]{3,0,2,1:T(8,128)(2,1)}, bf16[64,1,3,128]{3,0,2,1:T(8,128)(2,1)}, u32[]{:S(2)}, u32[]{:S(2)}) collective-permute-start(bf16[64,1,3,128]{3,0,2,1:T(8,128)(2,1)} %get-tuple-element.136), channel_id=1, source_target_pairs={{0,4},{2,6},{4,0},{6,2},{8,12},{10,14},{12,8},{14,10},{16,20},{18,... | collective-permute-start | bytes 147464 | tf_op jit(solution)/shard_map/ppermute | solution.py:20
  15.4 21.4 %collective-permute-start.2 = (bf16[64,1,3,128]{3,0,2,1:T(8,128)(2,1)}, bf16[64,1,3,128]{3,0,2,1:T(8,128)(2,1)}, u32[]{:S(2)}, u32[]{:S(2)}) collective-permute-start(bf16[64,1,3,128]{3,0,2,1:T(8,128)(2,1)} %get-tuple-element.135), channel_id=1, source_target_pairs={{0,6},{2,4},{4,2},{6,0},{8,14},{10,12},{12,10},{14,8},{16,22},{18,... | collective-permute-start | bytes 147464 | tf_op jit(solution)/shard_map/ppermute | solution.py:20
  15.5 25.5 %collective-permute-start.3 = (bf16[64,1,3,128]{3,0,2,1:T(8,128)(2,1)}, bf16[64,1,3,128]{3,0,2,1:T(8,128)(2,1)}, u32[]{:S(2)}, u32[]{:S(2)}) collective-permute-start(bf16[64,1,3,128]{3,0,2,1:T(8,128)(2,1)} %get-tuple-element.134), channel_id=1, source_target_pairs={{0,8},{2,10},{4,12},{6,14},{8,0},{10,2},{12,4},{14,6},{16,24},{18,... | collective-permute-start | bytes 147464 | tf_op jit(solution)/shard_map/ppermute | solution.py:20
  17.4 26.5 %collective-permute-start.4 = (bf16[64,1,3,128]{3,0,2,1:T(8,128)(2,1)}, bf16[64,1,3,128]{3,0,2,1:T(8,128)(2,1)}, u32[]{:S(2)}, u32[]{:S(2)}) collective-permute-start(bf16[64,1,3,128]{3,0,2,1:T(8,128)(2,1)} %get-tuple-element.133), channel_id=1, source_target_pairs={{0,10},{2,8},{4,14},{6,12},{8,2},{10,0},{12,6},{14,4},{16,26},{18,... | collective-permute-start | bytes 147464 | tf_op jit(solution)/shard_map/ppermute | solution.py:20
  19.0 2.7 %copy-start.13 = (bf16[64,1,3,128]{3,0,2,1:T(8,128)(2,1)S(1)}, bf16[64,1,3,128]{3,0,2,1:T(8,128)(2,1)}, u32[]{:S(2)}) copy-start(bf16[64,1,3,128]{3,0,2,1:T(8,128)(2,1)} %get-tuple-element.132) | copy-start | bytes 147460
  19.1 6.5 %copy-start.12 = (bf16[64,1,3,128]{3,0,2,1:T(8,128)(2,1)S(1)}, bf16[64,1,3,128]{3,0,2,1:T(8,128)(2,1)}, u32[]{:S(2)}) copy-start(bf16[64,1,3,128]{3,0,2,1:T(8,128)(2,1)} %get-tuple-element.131) | copy-start | bytes 147460
  19.1 17.7 %copy-start.11 = (bf16[64,1,3,128]{3,0,2,1:T(8,128)(2,1)S(1)}, bf16[64,1,3,128]{3,0,2,1:T(8,128)(2,1)}, u32[]{:S(2)}) copy-start(bf16[64,1,3,128]{3,0,2,1:T(8,128)(2,1)} %get-tuple-element.130) | copy-start | bytes 147460
  19.1 21.9 %copy-start.10 = (bf16[64,1,3,128]{3,0,2,1:T(8,128)(2,1)S(1)}, bf16[64,1,3,128]{3,0,2,1:T(8,128)(2,1)}, u32[]{:S(2)}) copy-start(bf16[64,1,3,128]{3,0,2,1:T(8,128)(2,1)} %get-tuple-element.129) | copy-start | bytes 147460
  19.1 24.8 %copy-start.9 = (bf16[64,1,3,128]{3,0,2,1:T(8,128)(2,1)S(1)}, bf16[64,1,3,128]{3,0,2,1:T(8,128)(2,1)}, u32[]{:S(2)}) copy-start(bf16[64,1,3,128]{3,0,2,1:T(8,128)(2,1)} %get-tuple-element.128) | copy-start | bytes 147460
  19.1 29.5 %copy-start.8 = (bf16[64,1,3,128]{3,0,2,1:T(8,128)(2,1)S(1)}, bf16[64,1,3,128]{3,0,2,1:T(8,128)(2,1)}, u32[]{:S(2)}) copy-start(bf16[64,1,3,128]{3,0,2,1:T(8,128)(2,1)} %get-tuple-element.127) | copy-start | bytes 147460
  20.1 29.2 %copy-start.7 = (bf16[64,1,3,128]{3,0,2,1:T(8,128)(2,1)S(1)}, bf16[64,1,3,128]{3,0,2,1:T(8,128)(2,1)}, u32[]{:S(2)}) copy-start(bf16[64,1,3,128]{3,0,2,1:T(8,128)(2,1)} %get-tuple-element.126) | copy-start | bytes 147460
  20.1 41.5 %copy-start.6 = (bf16[64,1,3,128]{3,0,2,1:T(8,128)(2,1)S(1)}, bf16[64,1,3,128]{3,0,2,1:T(8,128)(2,1)}, u32[]{:S(2)}) copy-start(bf16[64,1,3,128]{3,0,2,1:T(8,128)(2,1)} %get-tuple-element.125) | copy-start | bytes 147460
  21.8 26.8 %collective-permute-start.5 = (bf16[64,1,3,128]{3,0,2,1:T(8,128)(2,1)S(1)}, bf16[64,1,3,128]{3,0,2,1:T(8,128)(2,1)S(1)}, u32[]{:S(2)}, u32[]{:S(2)}) collective-permute-start(bf16[64,1,3,128]{3,0,2,1:T(8,128)(2,1)S(1)} %copy-done.13), channel_id=1, source_target_pairs={{0,12},{2,14},{4,8},{6,10},{8,4},{10,6},{12,0},{14,2},{16,28},{18,... | collective-permute-start | bytes 147464 | tf_op jit(solution)/shard_map/ppermute | solution.py:20
  25.6 23.8 %collective-permute-start.6 = (bf16[64,1,3,128]{3,0,2,1:T(8,128)(2,1)S(1)}, bf16[64,1,3,128]{3,0,2,1:T(8,128)(2,1)S(1)}, u32[]{:S(2)}, u32[]{:S(2)}) collective-permute-start(bf16[64,1,3,128]{3,0,2,1:T(8,128)(2,1)S(1)} %copy-done.12), channel_id=1, source_target_pairs={{0,14},{2,12},{4,10},{6,8},{8,6},{10,4},{12,2},{14,0},{16,30},{18,... | collective-permute-start | bytes 147464 | tf_op jit(solution)/shard_map/ppermute | solution.py:20
  30.2 34.6 %all-to-all-start.1 = ((bf16[64,16,3,128]{3,0,2,1:T(8,128)(2,1)}), bf16[64,16,3,128]{3,0,2,1:T(8,128)(2,1)S(1)}, u32[]{:S(2)}, u32[]{:S(2)}) async-start(bf16[64,16,3,128]{3,0,2,1:T(8,128)(2,1)} %bitcast.31), calls=%async_computation.1 | async-start | bytes 1572864 | tf_op jit(solution)/shard_map/all_to_all | solution.py:104
  36.7 24.9 %collective-permute-start.7 = (bf16[64,1,3,128]{3,0,2,1:T(8,128)(2,1)S(1)}, bf16[64,1,3,128]{3,0,2,1:T(8,128)(2,1)S(1)}, u32[]{:S(2)}, u32[]{:S(2)}) collective-permute-start(bf16[64,1,3,128]{3,0,2,1:T(8,128)(2,1)S(1)} %copy-done.11), channel_id=1, source_target_pairs={{0,16},{2,18},{4,20},{6,22},{8,24},{10,26},{12,28},{14,30},{16,0},... | collective-permute-start | bytes 147464 | tf_op jit(solution)/shard_map/ppermute | solution.py:20
  41.0 24.0 %collective-permute-start.8 = (bf16[64,1,3,128]{3,0,2,1:T(8,128)(2,1)S(1)}, bf16[64,1,3,128]{3,0,2,1:T(8,128)(2,1)S(1)}, u32[]{:S(2)}, u32[]{:S(2)}) collective-permute-start(bf16[64,1,3,128]{3,0,2,1:T(8,128)(2,1)S(1)} %copy-done.10), channel_id=1, source_target_pairs={{0,18},{2,16},{4,22},{6,20},{8,26},{10,24},{12,30},{14,28},{16,2},... | collective-permute-start | bytes 147464 | tf_op jit(solution)/shard_map/ppermute | solution.py:20
  43.9 21.9 %collective-permute-start.9 = (bf16[64,1,3,128]{3,0,2,1:T(8,128)(2,1)S(1)}, bf16[64,1,3,128]{3,0,2,1:T(8,128)(2,1)S(1)}, u32[]{:S(2)}, u32[]{:S(2)}) collective-permute-start(bf16[64,1,3,128]{3,0,2,1:T(8,128)(2,1)S(1)} %copy-done.9), channel_id=1, source_target_pairs={{0,20},{2,22},{4,16},{6,18},{8,28},{10,30},{12,24},{14,26},{16,4},... | collective-permute-start | bytes 147464 | tf_op jit(solution)/shard_map/ppermute | solution.py:20
  48.6 21.0 %collective-permute-start.10 = (bf16[64,1,3,128]{3,0,2,1:T(8,128)(2,1)S(1)}, bf16[64,1,3,128]{3,0,2,1:T(8,128)(2,1)S(1)}, u32[]{:S(2)}, u32[]{:S(2)}) collective-permute-start(bf16[64,1,3,128]{3,0,2,1:T(8,128)(2,1)S(1)} %copy-done.8), channel_id=1, source_target_pairs={{0,22},{2,20},{4,18},{6,16},{8,30},{10,28},{12,26},{14,24},{16,6},... | collective-permute-start | bytes 147464 | tf_op jit(solution)/shard_map/ppermute | solution.py:20
  49.3 22.4 %collective-permute-start.11 = (bf16[64,1,3,128]{3,0,2,1:T(8,128)(2,1)S(1)}, bf16[64,1,3,128]{3,0,2,1:T(8,128)(2,1)S(1)}, u32[]{:S(2)}, u32[]{:S(2)}) collective-permute-start(bf16[64,1,3,128]{3,0,2,1:T(8,128)(2,1)S(1)} %copy-done.7), channel_id=1, source_target_pairs={{0,24},{2,26},{4,28},{6,30},{8,16},{10,18},{12,20},{14,22},{16,8},... | collective-permute-start | bytes 147464 | tf_op jit(solution)/shard_map/ppermute | solution.py:20
  61.6 10.7 %collective-permute-start.12 = (bf16[64,1,3,128]{3,0,2,1:T(8,128)(2,1)S(1)}, bf16[64,1,3,128]{3,0,2,1:T(8,128)(2,1)S(1)}, u32[]{:S(2)}, u32[]{:S(2)}) collective-permute-start(bf16[64,1,3,128]{3,0,2,1:T(8,128)(2,1)S(1)} %copy-done.6), channel_id=1, source_target_pairs={{0,26},{2,24},{4,30},{6,28},{8,18},{10,16},{12,22},{14,20},{16,10}... | collective-permute-start | bytes 147464 | tf_op jit(solution)/shard_map/ppermute | solution.py:20
  64.8 1.0 copy-start.5
  64.8 4.8 %copy-start.4 = (bf16[64,1,3,128]{3,0,2,1:T(8,128)(2,1)S(1)}, bf16[64,1,3,128]{3,0,2,1:T(8,128)(2,1)}, u32[]{:S(2)}) copy-start(bf16[64,1,3,128]{3,0,2,1:T(8,128)(2,1)} %get-tuple-element.123) | copy-start | bytes 147460
  65.0 12.8 %collective-permute-start.15 = (bf16[2,3,1024,128]{3,2,1,0:T(8,128)(2,1)S(1)}, bf16[2,3,1024,128]{3,2,1,0:T(8,128)(2,1)S(1)}, u32[]{:S(2)}, u32[]{:S(2)}) collective-permute-start(bf16[2,3,1024,128]{3,2,1,0:T(8,128)(2,1)S(1)} %pad_maximum_fusion), channel_id=1, source_target_pairs={{0,1},{1,0},{2,3},{3,2},{4,5},{5,4},{6,7},{7,6},{8,9},{9,8},{10,11... | collective-permute-start | bytes 4718600 | tf_op jit(solution)/shard_map/ppermute | solution.py:28
  65.8 7.2 %collective-permute-start.13 = (bf16[64,1,3,128]{3,0,2,1:T(8,128)(2,1)S(1)}, bf16[64,1,3,128]{3,0,2,1:T(8,128)(2,1)S(1)}, u32[]{:S(2)}, u32[]{:S(2)}) collective-permute-start(bf16[64,1,3,128]{3,0,2,1:T(8,128)(2,1)S(1)} %copy-done.5), channel_id=1, source_target_pairs={{0,28},{2,30},{4,24},{6,26},{8,20},{10,22},{12,16},{14,18},{16,12}... | collective-permute-start | bytes 147464 | tf_op jit(solution)/shard_map/ppermute | solution.py:20
  69.5 7.7 %collective-permute-start.14 = (bf16[64,1,3,128]{3,0,2,1:T(8,128)(2,1)S(1)}, bf16[64,1,3,128]{3,0,2,1:T(8,128)(2,1)S(1)}, u32[]{:S(2)}, u32[]{:S(2)}) collective-permute-start(bf16[64,1,3,128]{3,0,2,1:T(8,128)(2,1)S(1)} %copy-done.4), channel_id=1, source_target_pairs={{0,30},{2,28},{4,26},{6,24},{8,22},{10,20},{12,18},{14,16},{16,14}... | collective-permute-start | bytes 147464 | tf_op jit(solution)/shard_map/ppermute | solution.py:20
  84.8 1.0 copy-start.1
  88.4 1.0 copy-start.1
  96.3 1.0 copy-start.1
  99.9 1.0 copy-start.1
  107.8 1.0 copy-start.1
  111.4 1.0 copy-start.1
